TPU v7x, 32 devices: a whole 2x2x4 slice. The times are simulated.
32 devices in a mesh: site: 2 (over x), row: 4 (over z), col: 4 (over y, core).
Axes of the slice: x: 2, y: 2, z: 4, core: 2. Of those that a mesh axis runs over, the one named last changes fastest.
Arguments:
- pair_array: bfloat16 [128, 64, 128], P(('site', 'row'), 'col'), parts along dimension 0, may hold values from -6 to 6
- in_gain: float32 [128], replicated, may hold values from 0.25 to 1.75
- left_weight: bfloat16 [256, 128], P('site'), parts along dimension 0, may hold values from -0.5 to 0.5
- right_weight: bfloat16 [256, 128], P('site'), parts along dimension 0, may hold values from -0.5 to 0.5
- mid_gain: float32 [128], replicated, may hold values from 0.25 to 1.75
- out_weight: bfloat16 [256, 128], P('site'), parts along dimension 0, may hold values from -0.5 to 0.5
- out_gate: bfloat16 [256, 128], P('site'), parts along dimension 0, may hold values from -0.5 to 0.5
Outputs:
- triangle_out: bfloat16 [128, 64, 128], P(('site', 'row'), 'col'), parts along dimension 0
There are 2 independent parts, one for each index of `site`. A program takes and returns all parts, laid end to end along the dimension named above; an argument that names none is the same for every part. Nothing has to cross between parts.
All inputs are finite; a program needn't handle non-finite values.
Results may differ from a plain program's by a relative error of at most 0.012.
Values may be sent and summed in bfloat16 or wider, within the bound.
A program may use at most 64 MiB of HBM per device.

v0:
```python
import jax
import jax.numpy as jnp
from jax import lax
from jax.sharding import PartitionSpec as P


def norm_channels(values, channel_gain):
    centred = values - jnp.mean(values, axis=-1, keepdims=True)
    return (
        centred
        * lax.rsqrt(jnp.mean(centred * centred, axis=-1, keepdims=True) + 1e-05)
        * channel_gain
    )


def both_factors(pair_in, in_gain, left_weight, right_weight):
    ready = norm_channels(pair_in.astype(jnp.float32), in_gain).astype(jnp.bfloat16)
    ready = lax.optimization_barrier(ready)
    left = jnp.einsum("ijc,cd->ijd", ready, left_weight, preferred_element_type=jnp.float32)
    right = jnp.einsum("ijc,cd->ijd", ready, right_weight, preferred_element_type=jnp.float32)
    return (ready, left.astype(jnp.bfloat16), right.astype(jnp.bfloat16))


def finish_pair(mixed, ready, mid_gain, out_weight, out_gate):
    scaled = norm_channels(mixed.astype(jnp.float32), mid_gain).astype(jnp.bfloat16)
    scaled = lax.optimization_barrier(scaled)
    gate = jax.nn.sigmoid(
        jnp.einsum("ijc,cd->ijd", ready, out_gate, preferred_element_type=jnp.float32)
    )
    return (
        jnp.einsum("ijd,dc->ijc", scaled, out_weight, preferred_element_type=jnp.float32) * gate
    ).astype(jnp.bfloat16)


def body(pair_array, in_gain, left_weight, right_weight, mid_gain, out_weight, out_gate):
    ready, left, right = both_factors(pair_array, in_gain, left_weight, right_weight)
    count = pair_array.shape[0] * lax.axis_size("row")
    left_lines, right_lines = (
        lax.all_to_all(left, "row", split_axis=2, concat_axis=0, tiled=True),
        lax.all_to_all(right, "row", split_axis=2, concat_axis=0, tiled=True),
    )
    strip = jnp.einsum(
        "kid,kjd->ijd",
        lax.all_gather(left_lines, "col", axis=1, tiled=True),
        right_lines,
        preferred_element_type=jnp.float32,
    )
    strip = (strip * count ** (-0.5)).astype(jnp.bfloat16)
    mixed = lax.all_to_all(strip, "row", split_axis=0, concat_axis=2, tiled=True)
    return finish_pair(mixed, ready, mid_gain, out_weight, out_gate)


def solution(mesh):
    return jax.shard_map(
        body,
        mesh=mesh,
        in_specs=(
            P(("site", "row"), "col", None),
            P(),
            P("site", None),
            P("site", None),
            P(),
            P("site", None),
            P("site", None),
        ),
        out_specs=P(("site", "row"), "col", None),
        check_vma=False,
    )
```

profile of v0, /device:TPU:0, one launch (start us, length us, event | category | flops | bytes accessed | tf_op | source)
XLA Modules:
  0.0 46.4 jit_solution(6474242782185736790)
XLA Ops:
  0.0 1.0 %convert_reduce_fusion = f32[16,16]{1,0:T(8,128)S(1)} fusion(bf16[16,16,128]{2,1,0:T(8,128)(2,1)} %param.7), kind=kLoop, calls=%fused_computation.15 | loop fusion | flops 65280 | bytes 66560 | tf_op jit(solution)/shard_map/reduce_sum | solution.py:8
  1.3 0.6 %copy-done.4 = f32[128]{0:T(128)S(1)} copy-done((f32[128]{0:T(128)S(1)}, f32[128]{0:T(128)}, u32[]{:S(2)}) %copy-start.4) | copy-done | bytes 536
  2.2 0.4 copy.32
  2.6 1.2 %reshape.39 = bf16[4,2,4096]{2,1,0:T(2,128)(2,1)} reshape(bf16[128,16,16]{2,1,0:T(8,128)(2,1)S(1)} %bitcast.43) | data formatting | bytes 131072
  3.8 6.5 %all-to-all-start = ((bf16[4,2,4096]{2,1,0:T(2,128)(2,1)}), bf16[4,2,4096]{2,1,0:T(2,128)(2,1)S(1)}, u32[]{:S(2)}, u32[]{:S(2)}) async-start(bf16[4,2,4096]{2,1,0:T(2,128)(2,1)} %reshape.39), calls=%async_computation | async-start | bytes 131072 | tf_op jit(solution)/shard_map/all_to_all | solution.py:40
  10.4 0.4 copy.34
  10.9 1.2 %reshape.41 = bf16[4,2,4096]{2,1,0:T(2,128)(2,1)} reshape(bf16[128,16,16]{2,1,0:T(8,128)(2,1)S(1)} %bitcast.44) | data formatting | bytes 131072
  12.0 4.0 %all-to-all-done = bf16[4,2,4096]{2,1,0:T(2,128)(2,1)S(1)} async-done(((bf16[4,2,4096]{2,1,0:T(2,128)(2,1)}), bf16[4,2,4096]{2,1,0:T(2,128)(2,1)S(1)}, u32[]{:S(2)}, u32[]{:S(2)}) %all-to-all-start) | async-done | bytes 65568 | tf_op jit(solution)/shard_map/all_to_all | solution.py:40
  16.0 3.3 %all-to-all-start.1 = ((bf16[4,2,4096]{2,1,0:T(2,128)(2,1)}), bf16[4,2,4096]{2,1,0:T(2,128)(2,1)S(1)}, u32[]{:S(2)}, u32[]{:S(2)}) async-start(bf16[4,2,4096]{2,1,0:T(2,128)(2,1)} %reshape.41), calls=%async_computation.1 | async-start | bytes 131072 | tf_op jit(solution)/shard_map/all_to_all | solution.py:39
  19.3 0.4 reshape.40
  19.7 0.4 copy.33
  20.2 0.3 copy.37
  20.5 4.6 %all-to-all-done.1 = bf16[4,2,4096]{2,1,0:T(2,128)(2,1)S(1)} async-done(((bf16[4,2,4096]{2,1,0:T(2,128)(2,1)}), bf16[4,2,4096]{2,1,0:T(2,128)(2,1)S(1)}, u32[]{:S(2)}, u32[]{:S(2)}) %all-to-all-start.1) | async-done | bytes 65568 | tf_op jit(solution)/shard_map/all_to_all | solution.py:39
  25.0 0.4 reshape.42
  25.4 0.4 copy.35
  25.9 0.3 copy.36
  26.2 7.2 %all_gather.3 = bf16[64,64,32]{0,1,2:T(8,128)(2,1)S(1)} all-gather(bf16[64,16,32]{0,1,2:T(8,128)(2,1)S(1)} %copy.36), channel_id=1, replica_groups=mesh['site'=2,'row'=4,'col'=4] {'col'}, dimensions={1}, use_global_device_ids=true | all-gather | bytes 327680 | tf_op jit(solution)/shard_map/all_gather | solution.py:44
  33.4 0.4 fusion.1
  34.4 8.1 %all_to_all.45 = bf16[4,2,4096]{2,1,0:T(2,128)(2,1)S(1)} all-to-all(bf16[4,2,4096]{2,1,0:T(2,128)(2,1)S(1)} %reshape.43), channel_id=1, replica_groups=mesh['site'=2,'row'=4,'col'=4] {'row'}, dimensions={0} | all-to-all | bytes 131072 | tf_op jit(solution)/shard_map/all_to_all | solution.py:49
  43.1 0.3 copy.39
  43.7 0.4 copy-done.5
  44.2 0.6 %copy-done.3 = bf16[128,128]{1,0:T(8,128)(2,1)S(1)} copy-done((bf16[128,128]{1,0:T(8,128)(2,1)S(1)}, bf16[128,128]{1,0:T(8,128)(2,1)}, u32[]{:S(2)}) %copy-start.3) | copy-done | bytes 32792
  45.0 0.6 %copy-done.6 = bf16[128,128]{1,0:T(8,128)(2,1)S(1)} copy-done((bf16[128,128]{1,0:T(8,128)(2,1)S(1)}, bf16[128,128]{1,0:T(8,128)(2,1)}, u32[]{:S(2)}) %copy-start.6) | copy-done | bytes 32792
  45.6 0.8 %fusion.6 = bf16[16,16,128]{2,1,0:T(8,128)(2,1)} fusion(f32[16,16,128]{2,1,0:T(8,128)S(1)} %fusion.14, bf16[16,16,128]{2,1,0:T(8,128)(2,1)S(1)} %fusion.12, bf16[128,128]{1,0:T(8,128)(2,1)S(1)} %copy-done.6), kind=kOutput, calls=%fused_computation.8 | convolution fusion | flops 8552448 | bytes 294912 | tf_op jit(solution)/shard_map/ijc,cd->ijd/dot_general | solution.py:28
  (27 shorter events, 2.3 us)
Async XLA Ops:
  0.0 2.0 %copy-start = (bf16[128,128]{1,0:T(8,128)(2,1)S(1)}, bf16[128,128]{1,0:T(8,128)(2,1)}, u32[]{:S(2)}) copy-start(bf16[128,128]{1,0:T(8,128)(2,1)} %param.10) | copy-start | bytes 98308
  0.0 1.0 %copy-start.1 = (bf16[16,16,128]{2,1,0:T(8,128)(2,1)S(1)}, bf16[16,16,128]{2,1,0:T(8,128)(2,1)}, u32[]{:S(2)}) copy-start(bf16[16,16,128]{2,1,0:T(8,128)(2,1)} %param.7) | copy-start | bytes 196612
  1.2 0.7 %copy-start.4 = (f32[128]{0:T(128)S(1)}, f32[128]{0:T(128)}, u32[]{:S(2)}) copy-start(f32[128]{0:T(128)} %param.8) | copy-start | bytes 1540
  3.8 6.5 %copy-start.2 = (bf16[128,128]{1,0:T(8,128)(2,1)S(1)}, bf16[128,128]{1,0:T(8,128)(2,1)}, u32[]{:S(2)}) copy-start(bf16[128,128]{1,0:T(8,128)(2,1)} %param.9) | copy-start | bytes 98308
  3.8 12.2 %all-to-all-start = ((bf16[4,2,4096]{2,1,0:T(2,128)(2,1)}), bf16[4,2,4096]{2,1,0:T(2,128)(2,1)S(1)}, u32[]{:S(2)}, u32[]{:S(2)}) async-start(bf16[4,2,4096]{2,1,0:T(2,128)(2,1)} %reshape.39), calls=%async_computation | async-start | bytes 131072 | tf_op jit(solution)/shard_map/all_to_all | solution.py:40
  16.0 9.0 %all-to-all-start.1 = ((bf16[4,2,4096]{2,1,0:T(2,128)(2,1)}), bf16[4,2,4096]{2,1,0:T(2,128)(2,1)S(1)}, u32[]{:S(2)}, u32[]{:S(2)}) async-start(bf16[4,2,4096]{2,1,0:T(2,128)(2,1)} %reshape.41), calls=%async_computation.1 | async-start | bytes 131072 | tf_op jit(solution)/shard_map/all_to_all | solution.py:39
  43.4 0.7 %copy-start.5 = (f32[128]{0:T(128)S(1)}, f32[128]{0:T(128)}, u32[]{:S(2)}) copy-start(f32[128]{0:T(128)} %param.11) | copy-start | bytes 1540
  44.1 0.8 %copy-start.3 = (bf16[128,128]{1,0:T(8,128)(2,1)S(1)}, bf16[128,128]{1,0:T(8,128)(2,1)}, u32[]{:S(2)}) copy-start(bf16[128,128]{1,0:T(8,128)(2,1)} %param.12) | copy-start | bytes 98308
  44.9 0.8 %copy-start.6 = (bf16[128,128]{1,0:T(8,128)(2,1)S(1)}, bf16[128,128]{1,0:T(8,128)(2,1)}, u32[]{:S(2)}) copy-start(bf16[128,128]{1,0:T(8,128)(2,1)} %param.13) | copy-start | bytes 98308
where the time goes:
time: 47 us; the launch traced here: 46.4 us
  blocking collectives  15.3 us (33%)
  starting transfers between devices  9.76 us (21%)
  local copies, waits for them, and re-layouts  9.11 us (19%)
  waiting for transfers between devices  8.55 us (18%)
  other arithmetic  1.87 us (4%)
  matrix products  1.61 us (3%)
    all_to_all x1, blocking collectives, body(): lax.all_to_all(strip, 'row', split_axis=0, concat_axis=2, tiled=True)  8.11 us
    all_gather x1, blocking collectives, body(): lax.all_gather(left_lines, 'col', axis=1, tiled=True)  7.2 us
    all_to_all x1, starting transfers between devices, body(): lax.all_to_all(right, 'row', split_axis=2, concat_axis=0, tiled=True)  6.48 us
    unnamed x20, local copies, waits for them, and re-layouts  5.82 us
    all_to_all x1, waiting for transfers between devices, body(): lax.all_to_all(left, 'row', split_axis=2, concat_axis=0, tiled=True)  4.56 us
    all_to_all x1, waiting for transfers between devices, body(): lax.all_to_all(right, 'row', split_axis=2, concat_axis=0, tiled=True)  3.99 us
    all_to_all x1, starting transfers between devices, body(): lax.all_to_all(left, 'row', split_axis=2, concat_axis=0, tiled=True)  3.28 us
    reduce_sum x2, other arithmetic, norm_channels(): centred = values - jnp.mean(values, axis=-1, keepdims=True)  1.14 us
  transfers between devices with their start and end apart: 2, of which 2 were waited for; matrix products, arithmetic and copies ran while one was open for 6% of the time, Pallas kernels for 0%

commit v1 on v0

--- a/solution.py
+++ b/solution.py
@@ -2,6 +2,24 @@
 import jax.numpy as jnp
 from jax import lax
 from jax.sharding import PartitionSpec as P
+
+
+def _get_stocks(mat, inp):
+    vec_out = jax.lax.axis_size("col")
+    fields = []
+    p_next, carry, formed = (vec_out, jax.lax.axis_index("col"), mat.shape[1])
+    for k0 in [*range(p_next)]:
+        x_now = (
+            jax.lax.ppermute(mat, "col", perm=[(w, (w + 1) % p_next) for w in range(p_next)])
+            if k0 + 1 < p_next
+            else mat
+        )
+        frame_out = inp(mat, (carry - k0) % p_next * formed)
+        fields.append(frame_out)
+        mat = x_now
+    work_now = jnp.concatenate(fields[::-1], axis=0)
+    e_now = jnp.roll(work_now, (carry + 1) * fields[0].shape[0], axis=0)
+    return e_now
 
 
 def norm_channels(values, channel_gain):
@@ -39,11 +57,11 @@
         lax.all_to_all(left, "row", split_axis=2, concat_axis=0, tiled=True),
         lax.all_to_all(right, "row", split_axis=2, concat_axis=0, tiled=True),
     )
-    strip = jnp.einsum(
-        "kid,kjd->ijd",
-        lax.all_gather(left_lines, "col", axis=1, tiled=True),
-        right_lines,
-        preferred_element_type=jnp.float32,
+    strip = _get_stocks(
+        left_lines,
+        lambda own_block, at: jnp.einsum(
+            "kid,kjd->ijd", own_block, right_lines, preferred_element_type=jnp.float32
+        ),
     )
     strip = (strip * count ** (-0.5)).astype(jnp.bfloat16)
     mixed = lax.all_to_all(strip, "row", split_axis=0, concat_axis=2, tiled=True)

time: 47 us -> 54 us (1.15)
  waiting for transfers between devices: 8.55 us -> 21.2 us
  blocking collectives: 15.3 us -> 8.11 us
  local copies, waits for them, and re-layouts: 9.11 us -> 10.2 us
    ppermute x0 -> x3, waiting for transfers between devices: none -> 12.6 us  [_get_stocks(): jax.lax.ppermute(mat, 'col', perm=[(w, (w + 1) % p_next) for w in range(p...]
    all_gather x1 -> x0, blocking collectives: 7.2 us -> none  [body(): lax.all_gather(left_lines, 'col', axis=1, tiled=True)]
    concatenate x0 -> x1, local copies, waits for them, and re-layouts: none -> 0.82 us  [_get_stocks(): e_now = jnp.roll(work_now, (carry + 1) * fields[0].shape[0], axis=0)]
  transfers between devices with their start and end apart: 2 -> 5, of which waited for: 2 -> 5; matrix products, arithmetic and copies ran while one was open for 6% -> 6% of each run, Pallas kernels for 0% -> 0%
where the time goes in v1:
time: 54 us; the launch traced here: 53.5 us
  waiting for transfers between devices  21.2 us (39%)
  local copies, waits for them, and re-layouts  10.2 us (19%)
  starting transfers between devices  9.82 us (18%)
  blocking collectives  8.11 us (15%)
  other arithmetic  2.01 us (4%)
  matrix products  1.92 us (4%)
    ppermute x3, waiting for transfers between devices, _get_stocks(): jax.lax.ppermute(mat, 'col', perm=[(w, (w + 1) % p_next) for w in range(p...  12.6 us
    all_to_all x1, blocking collectives, body(): lax.all_to_all(strip, 'row', split_axis=0, concat_axis=2, tiled=True)  8.11 us
    all_to_all x1, starting transfers between devices, body(): lax.all_to_all(right, 'row', split_axis=2, concat_axis=0, tiled=True)  6.48 us
    unnamed x20, local copies, waits for them, and re-layouts  6.06 us
    all_to_all x1, waiting for transfers between devices, body(): lax.all_to_all(left, 'row', split_axis=2, concat_axis=0, tiled=True)  4.54 us
    all_to_all x1, waiting for transfers between devices, body(): lax.all_to_all(right, 'row', split_axis=2, concat_axis=0, tiled=True)  4 us
    all_to_all x1, starting transfers between devices, body(): lax.all_to_all(left, 'row', split_axis=2, concat_axis=0, tiled=True)  3.28 us
    reduce_sum x2, other arithmetic, norm_channels(): centred = values - jnp.mean(values, axis=-1, keepdims=True)  1.14 us
  transfers between devices with their start and end apart: 5, of which 5 were waited for; matrix products, arithmetic and copies ran while one was open for 6% of the time, Pallas kernels for 0%

profile of v1, /device:TPU:0, one launch (start us, length us, event | category | flops | bytes accessed | tf_op | source)
XLA Modules:
  0.0 53.5 jit_solution(14726265388144336870)
XLA Ops:
  0.0 1.0 %convert_reduce_fusion = f32[16,16]{1,0:T(8,128)S(1)} fusion(bf16[16,16,128]{2,1,0:T(8,128)(2,1)} %param.7), kind=kLoop, calls=%fused_computation.17 | loop fusion | flops 65280 | bytes 66560 | tf_op jit(solution)/shard_map/reduce_sum | solution.py:26
  1.3 0.6 %copy-done.4 = f32[128]{0:T(128)S(1)} copy-done((f32[128]{0:T(128)S(1)}, f32[128]{0:T(128)}, u32[]{:S(2)}) %copy-start.4) | copy-done | bytes 536
  2.2 0.4 copy.44
  2.6 1.2 %reshape.39 = bf16[4,2,4096]{2,1,0:T(2,128)(2,1)} reshape(bf16[128,16,16]{2,1,0:T(8,128)(2,1)S(1)} %bitcast.55) | data formatting | bytes 131072
  3.8 6.5 %all-to-all-start = ((bf16[4,2,4096]{2,1,0:T(2,128)(2,1)}), bf16[4,2,4096]{2,1,0:T(2,128)(2,1)S(1)}, u32[]{:S(2)}, u32[]{:S(2)}) async-start(bf16[4,2,4096]{2,1,0:T(2,128)(2,1)} %reshape.39), calls=%async_computation | async-start | bytes 131072 | tf_op jit(solution)/shard_map/all_to_all | solution.py:58
  10.4 0.4 copy.46
  10.9 1.2 %reshape.41 = bf16[4,2,4096]{2,1,0:T(2,128)(2,1)} reshape(bf16[128,16,16]{2,1,0:T(8,128)(2,1)S(1)} %bitcast.56) | data formatting | bytes 131072
  12.0 4.0 %all-to-all-done = bf16[4,2,4096]{2,1,0:T(2,128)(2,1)S(1)} async-done(((bf16[4,2,4096]{2,1,0:T(2,128)(2,1)}), bf16[4,2,4096]{2,1,0:T(2,128)(2,1)S(1)}, u32[]{:S(2)}, u32[]{:S(2)}) %all-to-all-start) | async-done | bytes 65568 | tf_op jit(solution)/shard_map/all_to_all | solution.py:58
  16.0 3.3 %all-to-all-start.1 = ((bf16[4,2,4096]{2,1,0:T(2,128)(2,1)}), bf16[4,2,4096]{2,1,0:T(2,128)(2,1)S(1)}, u32[]{:S(2)}, u32[]{:S(2)}) async-start(bf16[4,2,4096]{2,1,0:T(2,128)(2,1)} %reshape.41), calls=%async_computation.1 | async-start | bytes 131072 | tf_op jit(solution)/shard_map/all_to_all | solution.py:57
  19.3 0.4 reshape.40
  19.7 0.4 copy.45
  20.5 4.5 %all-to-all-done.1 = bf16[4,2,4096]{2,1,0:T(2,128)(2,1)S(1)} async-done(((bf16[4,2,4096]{2,1,0:T(2,128)(2,1)}), bf16[4,2,4096]{2,1,0:T(2,128)(2,1)S(1)}, u32[]{:S(2)}, u32[]{:S(2)}) %all-to-all-start.1) | async-done | bytes 65568 | tf_op jit(solution)/shard_map/all_to_all | solution.py:57
  25.0 0.4 reshape.42
  25.4 0.4 copy.47
  26.4 4.2 %collective-permute-done = bf16[64,16,32]{0,1,2:T(8,128)(2,1)S(1)} collective-permute-done((bf16[64,16,32]{0,1,2:T(8,128)(2,1)S(1)}, bf16[64,16,32]{0,1,2:T(8,128)(2,1)S(1)}, u32[]{:S(2)}, u32[]{:S(2)}) %collective-permute-start) | collective-permute-done | bytes 65568 | tf_op jit(solution)/shard_map/ppermute | solution.py:13
  30.8 4.2 %collective-permute-done.1 = bf16[64,16,32]{0,1,2:T(8,128)(2,1)S(1)} collective-permute-done((bf16[64,16,32]{0,1,2:T(8,128)(2,1)S(1)}, bf16[64,16,32]{0,1,2:T(8,128)(2,1)S(1)}, u32[]{:S(2)}, u32[]{:S(2)}) %collective-permute-start.1) | collective-permute-done | bytes 65568 | tf_op jit(solution)/shard_map/ppermute | solution.py:13
  35.2 4.2 %collective-permute-done.2 = bf16[64,16,32]{0,1,2:T(8,128)(2,1)S(1)} collective-permute-done((bf16[64,16,32]{0,1,2:T(8,128)(2,1)S(1)}, bf16[64,16,32]{0,1,2:T(8,128)(2,1)S(1)}, u32[]{:S(2)}, u32[]{:S(2)}) %collective-permute-start.2) | collective-permute-done | bytes 65568 | tf_op jit(solution)/shard_map/ppermute | solution.py:13
  39.6 0.8 %concatenate.6 = f32[128,16,32]{0,1,2:T(8,128)S(1)} concatenate(f32[16,16,32]{0,1,2:T(8,128)S(1)} %convolution_bitcast_fusion.3, f32[16,16,32]{0,1,2:T(8,128)S(1)} %convolution_bitcast_fusion.2, f32[16,16,32]{0,1,2:T(8,128)S(1)} %convolution_bitcast_fusion.1, f32[16,16,32]{0,1,2:T(8,128)S(1)} %convolution_bitcast_fusion, f32[16,16,32]{0,1,2:T(8,128)S(1)} %convolution_bitcast_fusion.3, ...), dimensions={0} | concatenate | bytes 524288 | tf_op jit(solution)/shard_map/jit(_roll_dynamic)/concatenate | solution.py:21
  41.2 8.1 %all_to_all.45 = bf16[4,2,4096]{2,1,0:T(2,128)(2,1)S(1)} all-to-all(bf16[4,2,4096]{2,1,0:T(2,128)(2,1)S(1)} %reshape.43), channel_id=1, replica_groups=mesh['site'=2,'row'=4,'col'=4] {'row'}, dimensions={0} | all-to-all | bytes 131072 | tf_op jit(solution)/shard_map/all_to_all | solution.py:67
  49.5 0.3 copy.55
  50.5 0.6 %copy-done.5 = f32[128]{0:T(128)S(1)} copy-done((f32[128]{0:T(128)S(1)}, f32[128]{0:T(128)}, u32[]{:S(2)}) %copy-start.5) | copy-done | bytes 536
  51.3 0.6 %copy-done.3 = bf16[128,128]{1,0:T(8,128)(2,1)S(1)} copy-done((bf16[128,128]{1,0:T(8,128)(2,1)S(1)}, bf16[128,128]{1,0:T(8,128)(2,1)}, u32[]{:S(2)}) %copy-start.3) | copy-done | bytes 32792
  52.0 0.6 %copy-done.6 = bf16[128,128]{1,0:T(8,128)(2,1)S(1)} copy-done((bf16[128,128]{1,0:T(8,128)(2,1)S(1)}, bf16[128,128]{1,0:T(8,128)(2,1)}, u32[]{:S(2)}) %copy-start.6) | copy-done | bytes 32792
  52.6 0.8 %fusion.4 = bf16[16,16,128]{2,1,0:T(8,128)(2,1)} fusion(f32[16,16,128]{2,1,0:T(8,128)S(1)} %fusion.12, bf16[16,16,128]{2,1,0:T(8,128)(2,1)S(1)} %fusion.10, bf16[128,128]{1,0:T(8,128)(2,1)S(1)} %copy-done.6), kind=kOutput, calls=%fused_computation.9 | convolution fusion | flops 8552448 | bytes 294912 | tf_op jit(solution)/shard_map/ijc,cd->ijd/dot_general | solution.py:46
  (37 shorter events, 3.8 us)
Async XLA Ops:
  0.0 2.0 %copy-start = (bf16[128,128]{1,0:T(8,128)(2,1)S(1)}, bf16[128,128]{1,0:T(8,128)(2,1)}, u32[]{:S(2)}) copy-start(bf16[128,128]{1,0:T(8,128)(2,1)} %param.10) | copy-start | bytes 98308
  0.0 1.0 %copy-start.1 = (bf16[16,16,128]{2,1,0:T(8,128)(2,1)S(1)}, bf16[16,16,128]{2,1,0:T(8,128)(2,1)}, u32[]{:S(2)}) copy-start(bf16[16,16,128]{2,1,0:T(8,128)(2,1)} %param.7) | copy-start | bytes 196612
  1.2 0.7 %copy-start.4 = (f32[128]{0:T(128)S(1)}, f32[128]{0:T(128)}, u32[]{:S(2)}) copy-start(f32[128]{0:T(128)} %param.8) | copy-start | bytes 1540
  3.8 6.5 %copy-start.2 = (bf16[128,128]{1,0:T(8,128)(2,1)S(1)}, bf16[128,128]{1,0:T(8,128)(2,1)}, u32[]{:S(2)}) copy-start(bf16[128,128]{1,0:T(8,128)(2,1)} %param.9) | copy-start | bytes 98308
  3.8 12.2 %all-to-all-start = ((bf16[4,2,4096]{2,1,0:T(2,128)(2,1)}), bf16[4,2,4096]{2,1,0:T(2,128)(2,1)S(1)}, u32[]{:S(2)}, u32[]{:S(2)}) async-start(bf16[4,2,4096]{2,1,0:T(2,128)(2,1)} %reshape.39), calls=%async_computation | async-start | bytes 131072 | tf_op jit(solution)/shard_map/all_to_all | solution.py:58
  16.0 9.0 %all-to-all-start.1 = ((bf16[4,2,4096]{2,1,0:T(2,128)(2,1)}), bf16[4,2,4096]{2,1,0:T(2,128)(2,1)S(1)}, u32[]{:S(2)}, u32[]{:S(2)}) async-start(bf16[4,2,4096]{2,1,0:T(2,128)(2,1)} %reshape.41), calls=%async_computation.1 | async-start | bytes 131072 | tf_op jit(solution)/shard_map/all_to_all | solution.py:57
  26.2 4.4 %collective-permute-start = (bf16[64,16,32]{0,1,2:T(8,128)(2,1)S(1)}, bf16[64,16,32]{0,1,2:T(8,128)(2,1)S(1)}, u32[]{:S(2)}, u32[]{:S(2)}) collective-permute-start(bf16[64,16,32]{0,1,2:T(8,128)(2,1)S(1)} %copy.48), channel_id=1, source_target_pairs={{0,1},{1,2},{2,3},{3,0},{4,5},{5,6},{6,7},{7,4},{8,9},{9,10},{10,1... | collective-permute-start | bytes 196616 | tf_op jit(solution)/shard_map/ppermute | solution.py:13
  30.6 4.4 %collective-permute-start.1 = (bf16[64,16,32]{0,1,2:T(8,128)(2,1)S(1)}, bf16[64,16,32]{0,1,2:T(8,128)(2,1)S(1)}, u32[]{:S(2)}, u32[]{:S(2)}) collective-permute-start(bf16[64,16,32]{0,1,2:T(8,128)(2,1)S(1)} %collective-permute-done), channel_id=1, source_target_pairs={{0,1},{1,2},{2,3},{3,0},{4,5},{5,6},{6,7},{7,4},{8,9},{9,10},{10,1... | collective-permute-start | bytes 196616 | tf_op jit(solution)/shard_map/ppermute | solution.py:13
  35.0 4.4 %collective-permute-start.2 = (bf16[64,16,32]{0,1,2:T(8,128)(2,1)S(1)}, bf16[64,16,32]{0,1,2:T(8,128)(2,1)S(1)}, u32[]{:S(2)}, u32[]{:S(2)}) collective-permute-start(bf16[64,16,32]{0,1,2:T(8,128)(2,1)S(1)} %collective-permute-done.1), channel_id=1, source_target_pairs={{0,1},{1,2},{2,3},{3,0},{4,5},{5,6},{6,7},{7,4},{8,9},{9,10},{10,1... | collective-permute-start | bytes 196616 | tf_op jit(solution)/shard_map/ppermute | solution.py:13
  50.5 0.7 %copy-start.5 = (f32[128]{0:T(128)S(1)}, f32[128]{0:T(128)}, u32[]{:S(2)}) copy-start(f32[128]{0:T(128)} %param.11) | copy-start | bytes 1540
  51.1 0.8 %copy-start.3 = (bf16[128,128]{1,0:T(8,128)(2,1)S(1)}, bf16[128,128]{1,0:T(8,128)(2,1)}, u32[]{:S(2)}) copy-start(bf16[128,128]{1,0:T(8,128)(2,1)} %param.12) | copy-start | bytes 98308
  51.9 0.8 %copy-start.6 = (bf16[128,128]{1,0:T(8,128)(2,1)S(1)}, bf16[128,128]{1,0:T(8,128)(2,1)}, u32[]{:S(2)}) copy-start(bf16[128,128]{1,0:T(8,128)(2,1)} %param.13) | copy-start | bytes 98308
